TPU v7x, 32 devices: a whole 2x2x4 slice. The times are simulated.
32 devices in a mesh: batch: 8 (over z, y), vocab: 4 (over x, core).
Axes of the slice: x: 2, y: 2, z: 4, core: 2. Of those that a mesh axis runs over, the one named last changes fastest.
Arguments:
- hidden: bfloat16 [4096, 3584], P(('batch', 'vocab')), may hold values from -6 to 6
- head_weight: bfloat16 [3072, 3584], P('vocab', 'batch'), may hold values from -0.3125 to 0.3125
- targets: int32 [4096], P(('batch', 'vocab')), may hold values from 0 to 3071
- valid_mask: int32 [4096], P(('batch', 'vocab')), may hold values 0 or 1
Outputs:
- head_grad: float32 [3072, 3584], P('vocab', 'batch')
- hidden_grad: float32 [4096, 3584], P(('batch', 'vocab'))
- mean_loss: float32 [], replicated
All inputs are finite; a program needn't handle non-finite values. No bound on the sum of `valid_mask` on one device may be relied on, other than what follows from the above.
Results may differ from a plain program's by a relative error of at most 0.0019.
Values may be sent and summed in bfloat16 or wider, within the bound.
A program may use at most 128 MiB of HBM per device.

v0:
```python
import jax
import jax.numpy as jnp
from jax import lax
from jax.sharding import PartitionSpec as P

softcap = 30.0


def capped(scores):
    return softcap * jnp.tanh(scores / softcap)


def local(hidden, head_weight, targets, valid_mask):
    own_rows = head_weight.shape[0]
    batch_count = lax.axis_size("batch")
    vocab_index = lax.axis_index("vocab")
    group_ids, group_mask = (
        lax.all_gather(targets, "vocab", axis=0, tiled=True),
        lax.all_gather(valid_mask, "vocab", axis=0, tiled=True),
    )
    group_states = lax.all_gather(hidden, "vocab", axis=0, tiled=True)
    group_tokens = group_states.shape[0]
    first_row = vocab_index * own_rows
    inside = (group_ids >= first_row) & (group_ids < first_row + own_rows)
    local_index = jnp.where(inside, group_ids - first_row, -1)
    columns = jnp.arange(own_rows, dtype=jnp.int32)
    weight = group_mask.astype(jnp.float32)
    state_cols = group_states
    scores = lax.dot_general(
        state_cols,
        lax.all_gather(head_weight, "batch", axis=1, tiled=True),
        (((1,), (1,)), ((), ())),
        preferred_element_type=jnp.float32,
    )
    logits = capped(scores)
    target_hit = columns[None, :] == local_index[:, None]
    exponent = jnp.exp(logits)
    partition, target_logit = lax.psum(
        (jnp.sum(exponent, axis=1), jnp.sum(jnp.where(target_hit, logits, 0.0), axis=1)), "vocab"
    )
    slope = 1.0 - (logits / softcap) ** 2
    delta_logit = (
        weight[:, None] * (exponent / partition[:, None] - target_hit.astype(jnp.float32)) * slope
    ).astype(jnp.bfloat16)
    state_cols = group_states
    grad_columns = lax.psum_scatter(
        lax.dot_general(
            state_cols, delta_logit, (((0,), (0,)), ((), ())), preferred_element_type=jnp.float32
        ),
        "batch",
        scatter_dimension=0,
        tiled=True,
    )
    head_grad = jnp.transpose(grad_columns)
    partial_grad = jnp.dot(
        delta_logit,
        lax.all_gather(head_weight, "batch", axis=1, tiled=True),
        preferred_element_type=jnp.float32,
    )
    hidden_grad = lax.psum_scatter(partial_grad, "vocab", scatter_dimension=0, tiled=True)
    token_loss = weight * (jnp.log(partition) - target_logit)
    total_tokens = group_tokens * batch_count
    loss_total = lax.psum(jnp.sum(token_loss), "batch")
    mean_loss = loss_total / total_tokens
    return (head_grad, hidden_grad, mean_loss)


def solution(mesh):
    placed = (
        P(("batch", "vocab"), None),
        P("vocab", "batch"),
        P(("batch", "vocab")),
        P(("batch", "vocab")),
    )
    return jax.shard_map(
        local,
        mesh=mesh,
        in_specs=placed,
        out_specs=(P("vocab", "batch"), P(("batch", "vocab"), None), P()),
        check_vma=False,
    )
```

profile of v0, /device:TPU:0, one launch (start us, length us, event | category | flops | bytes accessed | tf_op | source)
XLA Modules:
  0.0 417.8 jit_solution(7849890568541200374)
XLA Ops:
  7.2 0.0 copy-start
  7.2 0.0 copy-start.1
  7.2 0.0 all-gather.5.cloned.1.call-start
  7.2 0.7 all-gather.5.cloned.1.call-update
  7.9 0.0 all-gather.7.cloned.1.call-start
  8.0 0.7 all-gather.7.cloned.1.call-update
  8.7 0.0 reduce-scatter.5.cloned.1.call-start
  8.7 6.0 %all-gather = s32[4,1,128]{2,1,0:T(1,128)S(1)} all-gather(s32[1,1,128]{2,1,0:T(1,128)S(1)} %bitcast.19), channel_id=1, replica_groups=mesh['batch'=8,'vocab'=4] {'vocab'}, dimensions={0}, use_global_device_ids=true | all-gather | bytes 2560 | tf_op jit(solution)/shard_map/all_gather | solution.py:19
  14.7 0.0 copy-done.1
  14.7 5.4 %all-gather.1 = s32[4,1,128]{2,1,0:T(1,128)S(1)} all-gather(s32[1,1,128]{2,1,0:T(1,128)S(1)} %bitcast.20), channel_id=1, replica_groups=mesh['batch'=8,'vocab'=4] {'vocab'}, dimensions={0}, use_global_device_ids=true | all-gather | bytes 2560 | tf_op jit(solution)/shard_map/all_gather | solution.py:18
  20.1 23.7 %all-gather.5.cloned.1.call-done = bf16[512,3584]{1,0:T(8,128)(2,1)} async-done(((bf16[128,3584]{1,0:T(8,128)(2,1)}), bf16[512,3584]{1,0:T(8,128)(2,1)}) %all-gather.5.cloned.1.call-update) | async-done | bytes 3670032 | tf_op jit(solution)/shard_map/all_gather | solution.py:21
  43.8 91.3 %all-gather.7.cloned.1.call-done = bf16[768,3584]{0,1:T(8,128)(2,1)} async-done(((bf16[768,448]{0,1:T(8,128)(2,1)}), bf16[768,3584]{0,1:T(8,128)(2,1)}) %all-gather.7.cloned.1.call-update) | async-done | bytes 5505040 | tf_op jit(solution)/shard_map/all_gather | solution.py:31
  135.1 7.0 %select_reduce_fusion = (f32[512]{0:T(512)S(1)}, f32[512]{0:T(512)S(1)}, f32[512,768]{1,0:T(8,128)S(1)}) fusion(s32[512]{0:T(512)S(1)} %bitcast.16, bf16[512,3584]{1,0:T(8,128)(2,1)} %all-gather.5.cloned.1.call-done, bf16[768,3584]{0,1:T(8,128)(2,1)} %all-gather.7.cloned.1.call-done), kind=kOutput, calls=%fused_computation.1 | convolution fusion | flops 2820930560 | bytes 10754048 | tf_op jit(solution)/shard_map/dot_general | solution.py:29
  142.1 5.7 %all-reduce = (f32[512]{0:T(512)S(1)}, f32[512]{0:T(512)S(1)}) all-reduce(f32[512]{0:T(512)S(1)} %get-tuple-element.10, f32[512]{0:T(512)S(1)} %get-tuple-element.9), channel_id=1, replica_groups=mesh['batch'=8,'vocab'=4] {'vocab'}, use_global_device_ids=true, to_apply=%region_1.2 | all-reduce | flops 1024 | bytes 8192 | tf_op jit(solution)/shard_map/psum | solution.py:38
  147.8 8.2 %fusion = f32[512,3584]{1,0:T(8,128)} fusion(bf16[768,3584]{0,1:T(8,128)(2,1)} %all-gather.7.cloned.1.call-done, f32[512,768]{1,0:T(8,128)S(1)} %get-tuple-element.13, s32[512]{0:T(512)S(1)} %bitcast.17, f32[512]{0:T(512)S(1)} %get-tuple-element.11, f32[512]{0:T(512)S(1)} %bitcast.13), kind=kOutput, calls=%fused_computation.8 | convolution fusion | flops 2822504448 | bytes 14424064 | tf_op jit(solution)/shard_map/dot_general | solution.py:55
  156.0 0.0 reduce-scatter.5.cloned.1.call-update
  156.0 0.0 reduce-scatter.7.cloned.1.call-start
  156.1 8.9 %convolution_bitcast_fusion = f32[3584,768]{0,1:T(8,128)} fusion(bf16[512,3584]{1,0:T(8,128)(2,1)} %all-gather.5.cloned.1.call-done, f32[512,768]{1,0:T(8,128)S(1)} %get-tuple-element.13, s32[512]{0:T(512)S(1)} %bitcast.18, f32[512]{0:T(512)S(1)} %get-tuple-element.11, f32[512]{0:T(512)S(1)} %bitcast.14), kind=kOutput, calls=%fused_computation | convolution fusion | flops 2822504448 | bytes 16259072 | tf_op jit(solution)/shard_map/dot_general | solution.py:47
  165.0 12.7 %copy.9 = f32[3584,768]{1,0:T(8,128)} copy(f32[3584,768]{0,1:T(8,128)} %convolution_bitcast_fusion) | data formatting | bytes 22020096
  177.7 0.0 reduce-scatter.7.cloned.1.call-update
  177.7 0.6 multiply_reduce_fusion
  178.3 19.4 %psum.23 = f32[]{:T(128)} all-reduce(f32[]{:T(128)} %multiply_reduce_fusion), channel_id=1, replica_groups=mesh['batch'=8,'vocab'=4] {'batch'}, use_global_device_ids=true, to_apply=%region_7.8 | all-reduce | flops 1 | bytes 8 | tf_op jit(solution)/shard_map/psum | solution.py:63
  198.4 22.1 %reduce-scatter.5.cloned.1.call-done = f32[128,3584]{1,0:T(8,128)} async-done(((f32[512,3584]{1,0:T(8,128)}), f32[128,3584]{1,0:T(8,128)}) %reduce-scatter.5.cloned.1.call-update) | async-done | bytes 1835024 | tf_op jit(solution)/shard_map/reduce_scatter | solution.py:60
  220.5 189.6 %reduce-scatter.7.cloned.1.call-done = f32[448,768]{1,0:T(8,128)} async-done(((f32[3584,768]{1,0:T(8,128)}), f32[448,768]{1,0:T(8,128)}) %reduce-scatter.7.cloned.1.call-update) | async-done | bytes 1376272
  (3 shorter events, 0.0 us)
Async XLA Ops:
  7.2 1.6 copy-start
  7.2 7.6 %copy-start.1 = (s32[128]{0:T(128)S(1)}, s32[128]{0:T(128)}, u32[]{:S(2)}) copy-start(s32[128]{0:T(128)} %param.6) | copy-start | bytes 1540
  7.2 36.6 %all-gather.5.cloned.1.call-start = ((), (), s32[]{:S(2)}) async-start(), calls=%async_computation.2 | async-start | bytes 4587520 | tf_op jit(solution)/shard_map/all_gather | solution.py:21
  7.9 127.2 %all-gather.7.cloned.1.call-start = ((), (), s32[]{:S(2)}) async-start(), calls=%async_computation.3 | async-start | bytes 6193152 | tf_op jit(solution)/shard_map/all_gather | solution.py:31
  8.7 211.9 %reduce-scatter.5.cloned.1.call-start = ((), (), s32[]{:S(2)}) async-start(), calls=%async_computation.4 | async-start | bytes 9175040 | tf_op jit(solution)/shard_map/reduce_scatter | solution.py:60
  156.0 254.1 %reduce-scatter.7.cloned.1.call-start = ((), (), s32[]{:S(2)}) async-start(), calls=%async_computation.5 | async-start | bytes 12386304
Sparse Core Ops, SparseCore 0:
  9.6 34.1 all-gather.4
  46.0 89.1 all-gather.6
  156.1 64.3 reduce-scatter.4
  224.6 185.4 reduce-scatter.6
where the time goes:
time: 418 us
  waiting for transfers between devices  328 us (78%)
  blocking collectives  36.5 us (9%)
  matrix products  24.1 us (6%)
  between operations  15.6 us (4%)
  local copies, waits for them, and re-layouts  12.7 us (3%)
    unnamed x5, waiting for transfers between devices  191 us
    all_gather x1, waiting for transfers between devices, local(): lax.all_gather(head_weight, 'batch', axis=1, tiled=True)  91.3 us
    all_gather x1, waiting for transfers between devices, local(): group_states = lax.all_gather(hidden, 'vocab', axis=0, tiled=True)  23.7 us
    reduce_scatter x1, waiting for transfers between devices, local(): lax.psum_scatter(partial_grad, 'vocab', scatter_dimension=0, tiled=True)  22.1 us
    psum x1, blocking collectives, local(): loss_total = lax.psum(jnp.sum(token_loss), 'batch')  19.4 us
    unnamed x5, local copies, waits for them, and re-layouts  12.7 us
    dot_general x1, matrix products, local(): lax.dot_general(state_cols, delta_logit, (((0,), (0,)), ((), ())), prefer...  8.94 us
  transfers between devices with their start and end apart: 4, of which 4 were waited for; matrix products, arithmetic and copies ran while one was open for 5% of the time, Pallas kernels for 0%

commit v1 on v0

v1 whole, which is shorter than its diff:
```python
import functools

import jax
import jax.numpy as jnp
from jax import lax
from jax.experimental import pallas as pl
from jax.experimental.pallas import tpu as pltpu
from jax.sharding import PartitionSpec as P

softcap = 30.0
MESH = pl.DeviceIdType.MESH
f32, bf16 = jnp.float32, jnp.bfloat16


def chunk_of(length, most):
    return max(s for s in range(16, most + 1, 16) if length % s == 0)


def kernel(sizes, h_in, w_in, code_in, head_out, hid_out, loss_out, h_all, w_all, code_all,
           logits, delta, stat_own, stat_all, loss_own, loss_all, grad, grad_send, y_in, z_out, z_in,
           part, core_in, x_out, x_in, *sems):
    nz, ny, nx, nv = sizes
    (own_sem, hs, hd, hr, ws_up, ws_dn, ws_y, wr, cs, cr, ss, sr, ls, lr,
     ys, yr, zs, zr, ds, dr, xs, xr) = sems
    nb = nz * ny
    rows, width = h_in.shape
    cols, entries = w_in.shape
    tokens = rows * nv
    b, v = lax.axis_index("batch"), lax.axis_index("vocab")
    z, y = lax.div(b, ny), lax.rem(b, ny)
    x, core = lax.div(v, 2), lax.rem(v, 2)
    other = x * 2 + 1 - core

    def at(bb, vv):
        return {"batch": bb, "vocab": vv}

    def copy(src, dst, send, recv, bb, vv):
        return pltpu.make_async_remote_copy(
            src_ref=src, dst_ref=dst, send_sem=send, recv_sem=recv, device_id=at(bb, vv), device_id_type=MESH)

    def hrow(i):
        return pl.ds(pl.multiple_of(i * rows, 16), rows)

    def wrow(i):
        return pl.ds(pl.multiple_of(i * cols, 16), cols)

    barrier = pltpu.get_barrier_semaphore()
    for k in range(1, nb):
        pl.semaphore_signal(barrier, inc=1, device_id=at(lax.rem(b + k, nb), v), device_id_type=MESH)
    for k in range(1, nv):
        pl.semaphore_signal(barrier, inc=1, device_id=at(b, lax.rem(v + k, nv)), device_id_type=MESH)
    pl.semaphore_wait(barrier, nb - 1 + nv - 1)

    def w_copy(zz, kind, k=0):
        i = zz * ny + y
        dst = w_all.at[wrow(i)]
        if kind == "up":
            return copy(dst, dst, ws_up.at[zz], wr.at[i], (z + 1) * ny + y, v)
        if kind == "down":
            return copy(dst, dst, ws_dn.at[zz], wr.at[i], (z - 1) * ny + y, v)
        return copy(dst, dst, ws_y.at[k - 1, zz], wr.at[i], z * ny + lax.rem(y + k, ny), v)

    def w_own(kind, k=0):
        dst = w_all.at[wrow(b)]
        if kind == "up":
            return copy(w_in, dst, ws_up.at[z], wr.at[b], b + ny, v)
        if kind == "down":
            return copy(w_in, dst, ws_dn.at[z], wr.at[b], b - ny, v)
        return copy(w_in, dst, ws_y.at[k - 1, z], wr.at[b], z * ny + lax.rem(y + k, ny), v)

    def h_x(k):
        return copy(h_in, h_all.at[hrow(v)], hs.at[k - 1], hr.at[v], b, lax.rem(x + k, nx) * 2 + core)

    def h_core(xx, own=False):
        i = xx * 2 + core
        dst = h_all.at[hrow(i)]
        return copy(h_in if own else dst, dst, hd.at[xx], hr.at[i], b, other)

    def code_copy(k):
        return copy(code_in, code_all.at[hrow(v)], cs.at[k - 1], cr.at[v], b, lax.rem(v + k, nv))

    for k in range(1, nv):
        code_copy(k).start()
    has_up, has_down = z + 1 < nz, z >= 1
    pl.when(has_up)(lambda: w_own("up").start())
    pl.when(has_down)(lambda: w_own("down").start())
    for k in range(1, ny):
        w_own("y", k).start()
    for k in range(1, nx):
        h_x(k).start()
    h_core(x, True).start()
    local = [
        pltpu.make_async_copy(w_in, w_all.at[wrow(b)], own_sem.at[0]),
        pltpu.make_async_copy(h_in, h_all.at[hrow(v)], own_sem.at[1]),
        pltpu.make_async_copy(code_in, code_all.at[hrow(v)], own_sem.at[2]),
    ]
    for one in local:
        one.start()

    for k in range(1, nz):
        @pl.when(z - k >= 0)
        def _():
            w_copy(z - k, "up").wait_recv()
            pl.when(has_up)(lambda: w_copy(z - k, "up").start())
            for j in range(1, ny):
                w_copy(z - k, "y", j).start()

        @pl.when(z + k < nz)
        def _():
            w_copy(z + k, "down").wait_recv()
            pl.when(has_down)(lambda: w_copy(z + k, "down").start())
            for j in range(1, ny):
                w_copy(z + k, "y", j).start()

        if k == 1:
            for j in range(1, nx):
                xx = lax.rem(x + j, nx)
                h_core(xx).wait_recv()
                h_core(xx).start()

    for one in local:
        one.wait()
    for j in range(nx):
        xx = lax.rem(x + j, nx)
        i = xx * 2 + 1 - core
        copy(h_in, h_all.at[hrow(i)], hd.at[xx], hr.at[i], b, other).wait_recv()
    for k in range(1, nv):
        i = lax.rem(v + k, nv)
        copy(code_in, code_all.at[hrow(i)], cs.at[k - 1], cr.at[i], b, i).wait_recv()
    for k in range(1, ny):
        yy = lax.rem(y + k, ny)
        for zz in range(nz):
            i = zz * ny + yy
            copy(w_in, w_all.at[wrow(i)], ws_y.at[k - 1, zz], wr.at[i], z * ny + yy, v).wait_recv()

    step = chunk_of(entries, 256)
    code = code_all[:, 0:1]
    weight = (code >= 0).astype(f32)

    def hits(n):
        ids = lax.broadcasted_iota(jnp.int32, (tokens, step), 1) + (v * entries + n * step)
        return ids == code

    def score_step(n, sums):
        total, hit_sum = sums
        span = pl.ds(pl.multiple_of(n * step, step), step)
        scores = jnp.dot(h_all[...], w_all[:, span], preferred_element_type=f32)
        capped = softcap * jnp.tanh(scores * (1.0 / softcap))
        logits[:, span] = capped
        total = total + jnp.sum(jnp.exp(capped), axis=1, keepdims=True)
        hit_sum = hit_sum + jnp.sum(jnp.where(hits(n), capped, 0.0), axis=1, keepdims=True)
        return total, hit_sum

    zero = jnp.zeros((tokens, 1), f32)
    total, hit_sum = lax.fori_loop(0, entries // step, score_step, (zero, zero))
    lane = lax.broadcasted_iota(jnp.int32, (tokens, 128), 1)
    turned = jnp.transpose(jnp.where(lane < 64, total, hit_sum))
    stat_own[...] = turned[56:72]

    def stat_copy(k):
        return copy(stat_own, stat_all.at[v], ss.at[k - 1], sr.at[v], b, lax.rem(v + k, nv))

    for k in range(1, nv):
        stat_copy(k).start()
    for k in range(1, nv):
        i = lax.rem(v + k, nv)
        copy(stat_own, stat_all.at[i], ss.at[k - 1], sr.at[i], b, i).wait_recv()
    stats = stat_own[...]
    for k in range(1, nv):
        stats = stats + stat_all[lax.rem(v + k, nv)]
    back = jnp.transpose(jnp.concatenate([stats[0:8]] * 8 + [stats[8:16]] * 8, axis=0))
    partition, target_logit = back[:, 0:1], back[:, 64:65]
    loss = jnp.sum(weight * (jnp.log(partition) - target_logit), axis=0, keepdims=True)
    loss_own[...] = jnp.broadcast_to(loss, loss_own.shape)

    def loss_copy(k):
        return copy(loss_own, loss_all.at[b], ls.at[k - 1], lr.at[b], lax.rem(b + k, nb), v)

    for k in range(1, nb):
        loss_copy(k).start()
    scale = weight / partition

    def delta_step(n, carry):
        span = pl.ds(pl.multiple_of(n * step, step), step)
        capped = logits[:, span]
        slope = 1.0 - (capped * (1.0 / softcap)) ** 2
        delta[:, span] = ((jnp.exp(capped) * scale - jnp.where(hits(n), weight, 0.0)) * slope).astype(bf16)
        return carry

    lax.fori_loop(0, entries // step, delta_step, 0)

    wide = chunk_of(width, 256)

    def grad_step(j, carry):
        span = pl.ds(pl.multiple_of(j * wide, wide), wide)
        share = lax.dot_general(h_all[:, span], delta[...], (((0,), (0,)), ((), ())), preferred_element_type=f32)
        grad[span, :] = share
        if grad_send is not None:
            grad_send[span, :] = share.astype(bf16)
        return carry

    lax.fori_loop(0, width // wide, grad_step, 0)
    y_src = grad if grad_send is None else grad_send

    def y_copy(k, zz):
        yy = lax.rem(y + k, ny)
        return copy(y_src.at[wrow(zz * ny + yy)], y_in.at[k - 1, zz], ys.at[k - 1, zz], yr.at[k - 1, zz],
                    z * ny + yy, v)

    order = [lax.rem(z + k, nz) for k in range(1, nz)] + [z]
    for zz in order:
        for k in range(1, ny):
            y_copy(k, zz).start()

    def part_step(j, carry):
        span = pl.ds(pl.multiple_of(j * wide, wide), wide)
        part[:, span] = lax.dot_general(
            delta[...], w_all[span, :], (((1,), (1,)), ((), ())), preferred_element_type=f32)
        return carry

    lax.fori_loop(0, width // wide, part_step, 0)

    def core_copy(xx):
        return copy(part.at[hrow(xx * 2 + 1 - core)], core_in.at[xx], ds.at[xx], dr.at[xx], b, other)

    def x_copy(k):
        return copy(x_out.at[k - 1], x_in.at[k - 1], xs.at[k - 1], xr.at[k - 1], b, lax.rem(x + k, nx) * 2 + core)

    xorder = [lax.rem(x + k, nx) for k in range(1, nx)] + [x]
    for xx in xorder:
        core_copy(xx).start()
    hstep = 16
    for k in range(1, nx + 1):
        xx = xorder[k - 1]
        core_copy(xx).wait_recv()

        def core_sum(r, carry):
            span = pl.ds(pl.multiple_of(r * hstep, hstep), hstep)
            mine = pl.ds(pl.multiple_of((xx * 2 + core) * rows + r * hstep, hstep), hstep)
            both = part[mine, :] + core_in[xx, span, :]
            if k < nx:
                x_out[k - 1, span, :] = both.astype(bf16)
            else:
                hid_out[span, :] = both
            return carry

        lax.fori_loop(0, rows // hstep, core_sum, 0)
        if k < nx:
            x_copy(k).start()

    cstep = chunk_of(cols, 64)

    def z_copy(k):
        zz = lax.rem(z + k, nz)
        return copy(z_out.at[k - 1], z_in.at[k - 1], zs.at[k - 1], zr.at[k - 1], zz * ny + y, v)

    for k in range(1, nz + 1):
        zz = order[k - 1]
        for j in range(1, ny):
            y_copy(j, zz).wait_recv()

        def y_sum(r, carry):
            span = pl.ds(pl.multiple_of(r * cstep, 16), cstep)
            total = grad[pl.ds(pl.multiple_of((zz * ny + y) * cols + r * cstep, 16), cstep), :]
            for j in range(1, ny):
                total = total + y_in[j - 1, zz, span, :].astype(f32)
            if k < nz:
                z_out[k - 1, span, :] = total.astype(bf16)
            else:
                head_out[span, :] = total
            return carry

        lax.fori_loop(0, cols // cstep, y_sum, 0)
        if k < nz:
            z_copy(k).start()

    for k in range(1, nx):
        x_copy(k).wait_recv()

        def x_sum(r, carry):
            span = pl.ds(pl.multiple_of(r * hstep, hstep), hstep)
            hid_out[span, :] += x_in[k - 1, span, :].astype(f32)
            return carry

        lax.fori_loop(0, rows // hstep, x_sum, 0)

    losses = loss_own[...]
    for k in range(1, nb):
        i = lax.rem(b + k, nb)
        copy(loss_own, loss_all.at[i], ls.at[k - 1], lr.at[i], i, v).wait_recv()
        losses = losses + loss_all[i]
    loss_out[...] = losses * (1.0 / (tokens * nb))

    for k in range(1, nz):
        z_copy(k).wait_recv()

        def z_sum(r, carry):
            span = pl.ds(pl.multiple_of(r * cstep, 16), cstep)
            head_out[span, :] += z_in[k - 1, span, :].astype(f32)
            return carry

        lax.fori_loop(0, cols // cstep, z_sum, 0)

    pl.when(has_up)(lambda: w_own("up").wait_send())
    pl.when(has_down)(lambda: w_own("down").wait_send())
    for k in range(1, ny):
        w_own("y", k).wait_send()
    for k in range(1, nz):
        @pl.when(z - k >= 0)
        def _():
            pl.when(has_up)(lambda: w_copy(z - k, "up").wait_send())
            for j in range(1, ny):
                w_copy(z - k, "y", j).wait_send()

        @pl.when(z + k < nz)
        def _():
            pl.when(has_down)(lambda: w_copy(z + k, "down").wait_send())
            for j in range(1, ny):
                w_copy(z + k, "y", j).wait_send()
        z_copy(k).wait_send()
    for k in range(1, nx):
        h_x(k).wait_send()
        h_core(lax.rem(x + k, nx)).wait_send()
        x_copy(k).wait_send()
    h_core(x, True).wait_send()
    for k in range(1, nv):
        code_copy(k).wait_send()
        stat_copy(k).wait_send()
    for k in range(1, nb):
        loss_copy(k).wait_send()
    for zz in order:
        for k in range(1, ny):
            y_copy(k, zz).wait_send()
    for xx in xorder:
        core_copy(xx).wait_send()


def local(nb, nv, hidden, head_weight, targets, valid_mask):
    nx = nv // 2
    ny = nx if nb % nx == 0 else 1
    nz = nb // ny
    rows, width = hidden.shape
    entries, cols = head_weight.shape
    tokens = rows * nv
    code = jnp.broadcast_to(jnp.where(valid_mask != 0, targets, -1)[:, None], (rows, 128))
    vm = pltpu.VMEM
    two = ny <= 2
    y_type = bf16 if two else f32
    dma = pltpu.SemaphoreType.DMA

    def some(n):
        return max(n, 1)

    buffers = [
        vm((tokens, width), bf16), vm((width, entries), bf16), vm((tokens, 128), jnp.int32),
        vm((tokens, entries), f32), vm((tokens, entries), bf16),
        vm((16, tokens), f32), vm((nv, 16, tokens), f32), vm((8, 128), f32), vm((nb, 8, 128), f32),
        vm((width, entries), f32), vm((width, entries) if two else (16, 128), bf16),
        vm((some(ny - 1), nz, cols, entries), y_type),
        vm((some(nz - 1), cols, entries), bf16), vm((some(nz - 1), cols, entries), bf16),
        vm((tokens, width), f32), vm((nx, rows, width), f32),
        vm((some(nx - 1), rows, width), bf16), vm((some(nx - 1), rows, width), bf16),
    ]
    sems = [
        dma((3,)), dma((some(nx - 1),)), dma((nx,)), dma((nv,)), dma((nz,)), dma((nz,)),
        dma((some(ny - 1), nz)), dma((nb,)), dma((nv,)), dma((nv,)), dma((nv,)), dma((nv,)), dma((nb,)), dma((nb,)),
        dma((some(ny - 1), nz)), dma((some(ny - 1), nz)), dma((nz,)), dma((nz,)), dma((nx,)), dma((nx,)),
        dma((nx,)), dma((nx,)),
    ]

    def body(*refs):
        refs = list(refs)
        if not two:
            refs[6 + 10] = None
        kernel((nz, ny, nx, nv), *refs)

    whole = pl.BlockSpec(memory_space=vm)
    head_t, hidden_grad, loss = pl.pallas_call(
        body,
        out_shape=(
            jax.ShapeDtypeStruct((cols, entries), f32),
            jax.ShapeDtypeStruct((rows, width), f32),
            jax.ShapeDtypeStruct((8, 128), f32),
        ),
        in_specs=[whole] * 3,
        out_specs=(whole,) * 3,
        scratch_shapes=buffers + sems,
        compiler_params=pltpu.CompilerParams(
            collective_id=0, has_side_effects=True, vmem_limit_bytes=67043328),
    )(hidden, jnp.transpose(head_weight), code)
    return jnp.transpose(head_t), hidden_grad, loss[0, 0]


def solution(mesh):
    placed = (
        P(("batch", "vocab"), None),
        P("vocab", "batch"),
        P(("batch", "vocab")),
        P(("batch", "vocab")),
    )
    return jax.shard_map(
        functools.partial(local, mesh.shape["batch"], mesh.shape["vocab"]),
        mesh=mesh,
        in_specs=placed,
        out_specs=(P("vocab", "batch"), P(("batch", "vocab"), None), P()),
        check_vma=False,
    )
```

time: 418 us -> 170 us (0.41)
  waiting for transfers between devices: 328 us -> 0 us
  Pallas kernels: 0 us -> 163 us
  blocking collectives: 36.5 us -> 0 us
  matrix products: 24.1 us -> 0 us
  between operations: 15.6 us -> 0.65 us
  local copies, waits for them, and re-layouts: 12.7 us -> 5.78 us
    unnamed x5 -> x0, waiting for transfers between devices: 191 us -> none
    pallas_call x0 -> x1, Pallas kernels: none -> 163 us  [local(): pl.pallas_call(body, out_shape=(jax.ShapeDtypeStruct((cols, entries), f32...]
    all_gather x2 -> x0, waiting for transfers between devices: 115 us -> none  [the longest x1 91.3 us: local(): lax.all_gather(head_weight, 'batch', axis=1, tiled=True)]
    psum x2 -> x0, blocking collectives: 25.1 us -> none  [the longest x1 19.4 us: local(): loss_total = lax.psum(jnp.sum(token_loss), 'batch')]
    dot_general x3 -> x0, matrix products: 24.1 us -> none  [the longest x1 8.94 us: local(): lax.dot_general(state_cols, delta_logit, (((0,), (0,)), ((), ())), prefer...]
    reduce_scatter x1 -> x0, waiting for transfers between devices: 22.1 us -> none  [local(): lax.psum_scatter(partial_grad, 'vocab', scatter_dimension=0, tiled=True)]
    all_gather x2 -> x0, blocking collectives: 11.4 us -> none  [the longest x1 6.01 us: local(): lax.all_gather(valid_mask, 'vocab', axis=0, tiled=True)]
    unnamed x5 -> x4, local copies, waits for them, and re-layouts: 12.7 us -> 3.74 us
  transfers between devices with their start and end apart: 4 -> 0, of which waited for: 4 -> 0; matrix products, arithmetic and copies ran while one was open for 5% -> 0% of each run, Pallas kernels for 0% -> 0%
where the time goes in v1:
time: 170 us
  Pallas kernels  163 us (96%)
  local copies, waits for them, and re-layouts  5.78 us (3%)
    pallas_call x1, Pallas kernels, local(): pl.pallas_call(body, out_shape=(jax.ShapeDtypeStruct((cols, entries), f32...  163 us
    unnamed x4, local copies, waits for them, and re-layouts  3.74 us

profile of v1, /device:TPU:0, one launch (start us, length us, event | category | flops | bytes accessed | tf_op | source)
XLA Modules:
  0.0 170.3 jit_solution(9696653243685908017)
XLA Ops:
  0.6 0.7 compare_select_fusion
  1.3 0.7 broadcast_in_dim.11.refs_2_
  2.0 163.2 %shard_map.67 = (f32[448,768]{1,0:T(8,128)}, f32[128,3584]{1,0:T(8,128)}, f32[8,128]{1,0:T(8,128)}) custom-call(bf16[128,3584]{1,0:T(8,128)(2,1)} %refs_0_.1, bf16[448,768]{1,0:T(8,128)(2,1)} %bitcast.4, s32[128,128]{1,0:T(8,128)} %broadcast_in_dim.11.refs_2_), custom_call_target="tpu_custom_call" | custom-call | tf_op jit(solution)/shard_map/pallas_call | solution.py:378
  165.2 0.0 copy-start
  165.2 1.3 slice.3
  166.5 2.5 %copy.9 = f32[768,448]{0,1:T(8,128)} copy(f32[768,448]{0,1:T(8,128)} %bitcast.3) | data formatting | bytes 2752512
  169.0 0.0 copy-done
  169.0 1.2 copy.10
Async XLA Ops:
  165.2 3.8 %copy-start = (f32[128,3584]{1,0:T(8,128)S(1)}, f32[128,3584]{1,0:T(8,128)}, u32[]{:S(2)}) copy-start(f32[128,3584]{1,0:T(8,128)} %get-tuple-element.13) | copy-start | bytes 5505028

commit v2 on v0

v2 whole, which is shorter than its diff:
```python
import functools

import jax
import jax.numpy as jnp
from jax import lax
from jax.experimental import pallas as pl
from jax.experimental.pallas import tpu as pltpu
from jax.sharding import PartitionSpec as P

softcap = 30.0
MESH = pl.DeviceIdType.MESH
f32, bf16 = jnp.float32, jnp.bfloat16


def chunk_of(length, most):
    return max(s for s in range(16, most + 1, 16) if length % s == 0)


def kernel(sizes, h_in, w_in, code_in, head_out, hid_out, loss_out, h_all, w_all, code_got, code_all,
           logits, delta, stat_own, stat_all, loss_own, loss_all, grad, grad_send, r_in,
           part, core_in, x_out, x_in, y_out, y_in, *sems):
    nz, ny, nx, nv = sizes
    (own_sem, hs, hf, hd, hr, ws_up, ws_dn, ws_y, wr, cs, cr, ss, sr, ls, lr,
     rs, rr, ds, dr, xs, xr, ys, yr) = sems
    nb = nz * ny
    rows, width = h_in.shape
    cols, half = w_in.shape[1:]
    group = ny * nv
    tokens = rows * group
    entries = ny * half
    b, v = lax.axis_index("batch"), lax.axis_index("vocab")
    z, y = lax.div(b, ny), lax.rem(b, ny)
    x, core = lax.div(v, 2), lax.rem(v, 2)
    other = x * 2 + 1 - core
    me = y * nv + v

    def at(bb, vv):
        return {"batch": bb, "vocab": vv}

    def copy(src, dst, send, recv, bb, vv):
        return pltpu.make_async_remote_copy(
            src_ref=src, dst_ref=dst, send_sem=send, recv_sem=recv, device_id=at(bb, vv), device_id_type=MESH)

    def hrow(i):
        return pl.ds(pl.multiple_of(i * rows, 16), rows)

    def wrow(i):
        return pl.ds(pl.multiple_of(i * cols, 16), cols)

    def turn_y(k):
        return lax.rem(y + k, ny)

    def turn_x(k):
        return lax.rem(x + k, nx)

    peers = [(k, j) for k in range(ny) for j in range(nv) if k or j]

    def peer(n):
        k, j = peers[n]
        return z * ny + turn_y(k), lax.rem(v + j, nv), turn_y(k) * nv + lax.rem(v + j, nv)

    barrier = pltpu.get_barrier_semaphore()
    for k in range(1, nb):
        pl.semaphore_signal(barrier, inc=1, device_id=at(lax.rem(b + k, nb), v), device_id_type=MESH)
    met = [n for n in range(len(peers)) if peers[n][1]]
    for n in met:
        bb, vv, _ = peer(n)
        pl.semaphore_signal(barrier, inc=1, device_id=at(bb, vv), device_id_type=MESH)
    pl.semaphore_wait(barrier, nb - 1 + len(met))

    def w_z(zz, yy, up, own=False):
        i = zz * ny + yy
        dst = w_all.at[wrow(i)]
        sem = (ws_up if up else ws_dn).at[i]
        return copy(w_in.at[y] if own else dst, dst, sem, wr.at[i], b + ny if up else b - ny, v)

    def w_y(k):
        return copy(w_in.at[turn_y(k)], w_all.at[wrow(b)], ws_y.at[k - 1], wr.at[b], z * ny + turn_y(k), v)

    def w_got(zz, yy):
        w_z(zz, yy, True).wait_recv()

    has_up, has_down = z + 1 < nz, z >= 1

    def h_send(n_src, sem, bb, vv, own=False):
        dst = h_all.at[hrow(n_src)]
        return copy(h_in if own else dst, dst, sem, hr.at[n_src], bb, vv)

    def h_x(k):
        return h_send(me, hs.at[k - 1], b, turn_x(k) * 2 + core, True)

    def h_y(k):
        return h_send(me, hs.at[nx + k - 1], z * ny + turn_y(k), v, True)

    def h_xy(kx, ky):
        return h_send(y * nv + turn_x(kx) * 2 + core, hf.at[kx, ky], z * ny + turn_y(ky), v)

    def h_yx(kx, ky):
        return h_send(turn_y(ky) * nv + v, hf.at[kx, ky], b, turn_x(kx) * 2 + core)

    def h_core(kx, ky):
        i = turn_y(ky) * nv + turn_x(kx) * 2 + core
        return h_send(i, hd.at[kx, ky], b, other, kx == 0 and ky == 0)

    def h_got(kx, ky, cc):
        i = turn_y(ky) * nv + turn_x(kx) * 2 + cc
        h_send(i, hd.at[kx, ky], b, other).wait_recv()

    def code_copy(n):
        bb, vv, _ = peer(n)
        return copy(code_in, code_got.at[me], cs.at[n], cr.at[me], bb, vv)

    for k in range(1, ny):
        w_y(k).start()
    pl.when(has_up)(lambda: w_z(z, y, True, True).start())
    pl.when(has_down)(lambda: w_z(z, y, False, True).start())
    for k in range(1, nx):
        h_x(k).start()
    for k in range(1, ny):
        h_y(k).start()
    for n in range(len(peers)):
        code_copy(n).start()
    h_core(0, 0).start()
    local = [
        pltpu.make_async_copy(w_in.at[y], w_all.at[wrow(b)], own_sem.at[0]),
        pltpu.make_async_copy(h_in, h_all.at[hrow(me)], own_sem.at[1]),
    ]
    for one in local:
        one.start()

    for k in range(1, ny):
        w_got(z, turn_y(k))
        pl.when(has_up)(lambda: w_z(z, turn_y(k), True).start())
        pl.when(has_down)(lambda: w_z(z, turn_y(k), False).start())

    def h_pass():
        for kx in range(1, nx):
            h_got(kx, 0, core)
            for ky in range(1, ny):
                pl.when(core == 0)(lambda: h_xy(kx, ky).start())
            h_core(kx, 0).start()
        for ky in range(1, ny):
            h_got(0, ky, core)
            for kx in range(1, nx):
                pl.when(core == 1)(lambda: h_yx(kx, ky).start())
            h_core(0, ky).start()

    def h_rest():
        for kx in range(1, nx):
            for ky in range(1, ny):
                h_got(kx, ky, core)
                h_core(kx, ky).start()

    for k in range(1, nz):
        for j in range(ny):
            yy = turn_y(j)

            @pl.when(z - k >= 0)
            def _():
                w_got(z - k, yy)
                pl.when(has_up)(lambda: w_z(z - k, yy, True).start())

            @pl.when(z + k < nz)
            def _():
                w_got(z + k, yy)
                pl.when(has_down)(lambda: w_z(z + k, yy, False).start())
        if k == 1:
            h_pass()
        if k == min(2, nz - 1):
            h_rest()

    for one in local:
        one.wait()
    for kx in range(nx):
        for ky in range(ny):
            h_got(kx, ky, 1 - core)
    code_got[me] = code_in[...]
    for n in range(len(peers)):
        bb, vv, i = peer(n)
        copy(code_in, code_got.at[i], cs.at[n], cr.at[i], bb, vv).wait_recv()
    for i in range(group):
        code_all[i * rows:(i + 1) * rows, :] = jnp.transpose(jnp.concatenate([code_got[i]] * 16, axis=0))

    step = chunk_of(tokens, 256)
    lanes = lax.broadcasted_iota(jnp.int32, (step, 128), 1)
    first = v * entries + y * half

    def span_of(n):
        return pl.ds(pl.multiple_of(n * step, step), step)

    def hits(n):
        ids = lax.broadcasted_iota(jnp.int32, (step, half), 1) + first
        return ids == code_all[span_of(n), 0:1].astype(jnp.int32)

    for n in range(tokens // step):
        span = pl.ds(n * step, step)
        scores = jnp.dot(h_all[span, :], w_all[...], preferred_element_type=f32)
        capped = softcap * jnp.tanh(scores * (1.0 / softcap))
        logits[span, :] = capped
        total = jnp.sum(jnp.exp(capped), axis=1, keepdims=True)
        hit_sum = jnp.sum(jnp.where(hits(n), capped, 0.0), axis=1, keepdims=True)
        turned = jnp.transpose(jnp.where(lax.rem(lanes, 8) < 4, total, hit_sum))
        stat_own[:, n * step:(n + 1) * step] = turned[0:8]

    def stat_copy(n):
        bb, vv, _ = peer(n)
        return copy(stat_own, stat_all.at[me], ss.at[n], sr.at[me], bb, vv)

    for n in range(len(peers)):
        stat_copy(n).start()
    for n in range(len(peers)):
        bb, vv, i = peer(n)
        copy(stat_own, stat_all.at[i], ss.at[n], sr.at[i], bb, vv).wait_recv()
    stats = stat_own[...]
    for n in range(len(peers)):
        stats = stats + stat_all[peer(n)[2]]

    loss = jnp.zeros((1, 1), f32)
    for n in range(tokens // step):
        span = pl.ds(n * step, step)
        weight = (code_all[span, 0:1] >= 0).astype(f32)
        back = jnp.transpose(jnp.concatenate([stats[:, n * step:(n + 1) * step]] * 16, axis=0))
        partition, target_logit = back[:, 0:1], back[:, 4:5]
        loss = loss + jnp.sum(weight * (jnp.log(partition) - target_logit), axis=0, keepdims=True)
        capped = logits[span, :]
        slope = 1.0 - (capped * (1.0 / softcap)) ** 2
        delta[span, :] = ((jnp.exp(capped) * (weight / partition) - jnp.where(hits(n), weight, 0.0)) * slope
                          ).astype(bf16)
    loss_own[...] = jnp.broadcast_to(loss, loss_own.shape)

    def loss_copy(k):
        return copy(loss_own, loss_all.at[b], ls.at[k - 1], lr.at[b], lax.rem(b + k, nb), v)

    def r_copy(zz, yy):
        i = zz * ny + yy
        return copy(grad_send.at[wrow(i)], r_in.at[z, y], rs.at[i], rr.at[b], i, v)

    def grad_share(span):
        return lax.dot_general(h_all[:, span], delta[...], (((0,), (0,)), ((), ())), preferred_element_type=f32)

    order = [lax.rem(z + k, nz) for k in range(1, nz)] + [z]
    slab = ny * cols
    if slab % 128 == 0:
        mine = y * cols
        for n in range(nz):
            zz = order[n]
            span = pl.ds(pl.multiple_of(zz * slab, 128), slab)
            share = grad_share(span)
            grad_send[span, :] = share.astype(bf16)
            if n == nz - 1:
                grad[...] = share
            for k in range(ny):
                if n < nz - 1 or k:
                    r_copy(zz, turn_y(k)).start()
    else:
        mine = b * cols
        wide = chunk_of(width, 256)

        def grad_step(j, carry):
            span = pl.ds(pl.multiple_of(j * wide, wide), wide)
            share = grad_share(span)
            grad[span, :] = share
            grad_send[span, :] = share.astype(bf16)
            return carry

        lax.fori_loop(0, width // wide, grad_step, 0)
        for n in range(nz):
            for k in range(ny):
                if n < nz - 1 or k:
                    r_copy(order[n], turn_y(k)).start()
    for k in range(1, nb):
        loss_copy(k).start()

    wide = chunk_of(width, 256)

    def part_step(j, carry):
        span = pl.ds(pl.multiple_of(j * wide, wide), wide)
        part[:, span] = lax.dot_general(
            delta[...], w_all[span, :], (((1,), (1,)), ((), ())), preferred_element_type=f32)
        return carry

    lax.fori_loop(0, width // wide, part_step, 0)

    def core_copy(kx, ky):
        i = turn_y(ky) * nv + turn_x(kx) * 2 + 1 - core
        return copy(part.at[hrow(i)], core_in.at[kx, ky], ds.at[kx, ky], dr.at[kx, ky], b, other)

    def x_copy(kx, ky):
        return copy(x_out.at[kx - 1, ky], x_in.at[kx - 1, ky], xs.at[kx, ky], xr.at[kx, ky],
                    b, turn_x(kx) * 2 + core)

    def y_copy(ky):
        return copy(y_out.at[ky - 1], y_in.at[ky - 1], ys.at[ky], yr.at[ky], z * ny + turn_y(ky), v)

    ways = [(kx % nx, ky % ny) for kx in range(1, nx + 1) for ky in range(1, ny + 1)]
    for kx, ky in ways:
        core_copy(kx, ky).start()
    hstep = 16

    def over_rows(start, body):
        def one(r, carry):
            body(pl.ds(pl.multiple_of(r * hstep, hstep), hstep),
                 pl.ds(pl.multiple_of(start + r * hstep, hstep), hstep))
            return carry

        lax.fori_loop(0, rows // hstep, one, 0)

    def start_of(kx, ky):
        return (turn_y(ky) * nv + turn_x(kx) * 2 + core) * rows

    for kx, ky in ways:
        core_copy(kx, ky).wait_recv()

        def core_sum(span, here):
            both = part[here, :] + core_in[kx, ky, span, :]
            if kx:
                x_out[kx - 1, ky, span, :] = both.astype(bf16)
            else:
                part[here, :] = both

        over_rows(start_of(kx, ky), core_sum)
        if kx:
            x_copy(kx, ky).start()

    for ky in [k % ny for k in range(1, ny + 1)]:
        for kx in range(1, nx):
            x_copy(kx, ky).wait_recv()

        def x_sum(span, here):
            total = part[here, :]
            for kx in range(1, nx):
                total = total + x_in[kx - 1, ky, span, :].astype(f32)
            if ky:
                y_out[ky - 1, span, :] = total.astype(bf16)
            else:
                hid_out[span, :] = total

        over_rows(start_of(0, ky), x_sum)
        if ky:
            y_copy(ky).start()

    cstep = chunk_of(cols, 64)

    def over_cols(body):
        def one(r, carry):
            body(pl.multiple_of(r * cstep, 16))
            return carry

        lax.fori_loop(0, cols // cstep, one, 0)

    def r_got(zz, yy):
        i = zz * ny + yy
        copy(grad_send.at[wrow(i)], r_in.at[zz, yy], rs.at[i], rr.at[i], i, v).wait_recv()

    for k in range(1, ny):
        r_got(z, turn_y(k))

    def first_sum(r):
        head_out[y, pl.ds(r, cstep), :] = grad[pl.ds(pl.multiple_of(mine + r, 16), cstep), :]
        for k in range(1, ny):
            head_out[turn_y(k), pl.ds(r, cstep), :] = r_in[z, turn_y(k), pl.ds(r, cstep), :].astype(f32)

    over_cols(first_sum)
    for n in range(1, nz):
        zz = lax.rem(z + nz - n, nz)
        for k in range(ny):
            r_got(zz, turn_y(k))
        if n == nz - 1:
            for ky in range(1, ny):
                y_copy(ky).wait_recv()

                def y_sum(span, here):
                    hid_out[span, :] += y_in[ky - 1, span, :].astype(f32)

                over_rows(0, y_sum)

        def more_sum(r):
            for k in range(ny):
                head_out[turn_y(k), pl.ds(r, cstep), :] += r_in[zz, turn_y(k), pl.ds(r, cstep), :].astype(f32)

        over_cols(more_sum)

    losses = loss_own[...]
    for k in range(1, nb):
        i = lax.rem(b + k, nb)
        copy(loss_own, loss_all.at[i], ls.at[k - 1], lr.at[i], i, v).wait_recv()
        losses = losses + loss_all[i]
    loss_out[...] = losses * (1.0 / (tokens * nb))

    for j in range(ny):
        yy = turn_y(j)
        pl.when(has_up)(lambda: w_z(z, yy, True, j == 0).wait_send())
        pl.when(has_down)(lambda: w_z(z, yy, False, j == 0).wait_send())
        for k in range(1, nz):
            @pl.when(z - k >= 0)
            def _():
                pl.when(has_up)(lambda: w_z(z - k, yy, True).wait_send())

            @pl.when(z + k < nz)
            def _():
                pl.when(has_down)(lambda: w_z(z + k, yy, False).wait_send())
    for k in range(1, ny):
        w_y(k).wait_send()
        h_y(k).wait_send()
        y_copy(k).wait_send()
    for k in range(1, nx):
        h_x(k).wait_send()
        for ky in range(1, ny):
            pl.when(core == 0)(lambda: h_xy(k, ky).wait_send())
            pl.when(core == 1)(lambda: h_yx(k, ky).wait_send())
    for kx, ky in ways:
        h_core(kx, ky).wait_send()
        core_copy(kx, ky).wait_send()
        if kx:
            x_copy(kx, ky).wait_send()
    for n in range(len(peers)):
        code_copy(n).wait_send()
        stat_copy(n).wait_send()
    for k in range(1, nb):
        loss_copy(k).wait_send()
    for n in range(nz):
        for k in range(ny):
            if n < nz - 1 or k:
                r_copy(order[n], turn_y(k)).wait_send()


def local(nb, nv, hidden, head_weight, targets, valid_mask):
    nx = nv // 2
    ny = nx if nx <= 2 and nb % nx == 0 else 1
    nz = nb // ny
    rows, width = hidden.shape
    entries, cols = head_weight.shape
    half = entries // ny
    group = ny * nv
    tokens = rows * group
    code = jnp.broadcast_to(jnp.where(valid_mask != 0, targets, -1).astype(f32)[None, :], (8, rows))
    weight = jnp.transpose(head_weight.reshape(ny, half, cols), (0, 2, 1))
    vm = pltpu.VMEM
    dma = pltpu.SemaphoreType.DMA
    slab = ny * cols
    ly, lx = max(ny - 1, 1), max(nx - 1, 1)
    buffers = [
        vm((tokens, width), bf16), vm((width, half), bf16), vm((group, 8, rows), f32), vm((tokens, 128), f32),
        vm((tokens, half), f32), vm((tokens, half), bf16),
        vm((8, tokens), f32), vm((group, 8, tokens), f32), vm((8, 128), f32), vm((nb, 8, 128), f32),
        vm((slab if slab % 128 == 0 else width, half), f32), vm((width, half), bf16), vm((nz, ny, cols, half), bf16),
        vm((tokens, width), f32), vm((nx, ny, rows, width), f32),
        vm((lx, ny, rows, width), bf16), vm((lx, ny, rows, width), bf16),
        vm((ly, rows, width), bf16), vm((ly, rows, width), bf16),
    ]
    sems = [
        dma((2,)), dma((nx + ny,)), dma((nx, ny)), dma((nx, ny)), dma((group,)), dma((nb,)), dma((nb,)),
        dma((ly,)), dma((nb,)), dma((group,)), dma((group,)), dma((group,)), dma((group,)), dma((nb,)), dma((nb,)),
        dma((nb,)), dma((nb,)), dma((nx, ny)), dma((nx, ny)), dma((nx, ny)), dma((nx, ny)), dma((ny,)), dma((ny,)),
    ]
    whole = pl.BlockSpec(memory_space=vm)
    head_t, hidden_grad, loss = pl.pallas_call(
        functools.partial(kernel, (nz, ny, nx, nv)),
        out_shape=(
            jax.ShapeDtypeStruct((ny, cols, half), f32),
            jax.ShapeDtypeStruct((rows, width), f32),
            jax.ShapeDtypeStruct((8, 128), f32),
        ),
        in_specs=[whole] * 3,
        out_specs=(whole,) * 3,
        scratch_shapes=buffers + sems,
        compiler_params=pltpu.CompilerParams(
            collective_id=0, has_side_effects=True, vmem_limit_bytes=67043328),
    )(hidden, weight, code)
    return jnp.transpose(head_t, (0, 2, 1)).reshape(entries, cols), hidden_grad, loss[0, 0]


def solution(mesh):
    placed = (
        P(("batch", "vocab"), None),
        P("vocab", "batch"),
        P(("batch", "vocab")),
        P(("batch", "vocab")),
    )
    return jax.shard_map(
        functools.partial(local, mesh.shape["batch"], mesh.shape["vocab"]),
        mesh=mesh,
        in_specs=placed,
        out_specs=(P("vocab", "batch"), P(("batch", "vocab"), None), P()),
        check_vma=False,
    )
```

time: 418 us -> 145 us (0.35)
  the two profiles are of different devices: /device:TPU:0 before, /device:TPU:24 now
where the time goes in v2:
time: 145 us
  Pallas kernels  136 us (94%)
  local copies, waits for them, and re-layouts  7.68 us (5%)
    pallas_call x1, Pallas kernels, local(): pl.pallas_call(functools.partial(kernel, (nz, ny, nx, nv)), out_shape=(ja...  136 us

profile of v2, /device:TPU:24, one launch (start us, length us, event | category | flops | bytes accessed | tf_op | source)
XLA Modules:
  0.0 144.6 jit_solution(14879353184341648705)
XLA Ops:
  0.6 0.7 fusion
  1.3 0.6 broadcast_in_dim.11.code_in
  1.9 2.0 %copy.12 = bf16[56,2,8,384]{3,2,0,1:T(8,128)(2,1)} copy(bf16[56,2,8,384]{3,2,1,0:T(8,128)(2,1)} %bitcast.14) | data formatting | bytes 1376256 | tf_op jit(solution)/shard_map/reshape | solution.py:437
  3.9 135.6 %shard_map.67 = (f32[2,448,384]{2,1,0:T(8,128)}, f32[128,3584]{1,0:T(8,128)}, f32[8,128]{1,0:T(8,128)}) custom-call(bf16[128,3584]{1,0:T(8,128)(2,1)} %h_in.1, bf16[2,448,384]{2,1,0:T(8,128)(2,1)} %bitcast.11, f32[8,128]{1,0:T(8,128)} %broadcast_in_dim.11.code_in), custom_call_target="tpu_custom_call" | custom-call | tf_op jit(solution)/shard_map/pallas_call | solution.py:457
  139.5 0.0 copy-start
  139.5 1.3 slice.3
  140.8 2.5 %copy.10 = f32[2,56,8,384]{3,2,0,1:T(8,128)} copy(f32[2,56,8,384]{3,2,1,0:T(8,128)} %bitcast.13) | data formatting | bytes 2752512 | tf_op jit(solution)/shard_map/reshape | solution.py:470
  143.3 0.0 copy-done
  143.3 1.2 copy.14
Async XLA Ops:
  139.5 3.9 %copy-start = (f32[128,3584]{1,0:T(8,128)S(1)}, f32[128,3584]{1,0:T(8,128)}, u32[]{:S(2)}) copy-start(f32[128,3584]{1,0:T(8,128)} %get-tuple-element.13) | copy-start | bytes 5505028

commit v3 on v2

--- a/solution.py
+++ b/solution.py
@@ -18,10 +18,10 @@
 
 def kernel(sizes, h_in, w_in, code_in, head_out, hid_out, loss_out, h_all, w_all, code_got, code_all,
            logits, delta, stat_own, stat_all, loss_own, loss_all, grad, grad_send, r_in,
-           part, core_in, x_out, x_in, y_out, y_in, *sems):
+           part, core_in, x_out, x_in, y_out, y_in, far_own, far_in, *sems):
     nz, ny, nx, nv = sizes
     (own_sem, hs, hf, hd, hr, ws_up, ws_dn, ws_y, wr, cs, cr, ss, sr, ls, lr,
-     rs, rr, ds, dr, xs, xr, ys, yr) = sems
+     rs, rr, ds, dr, xs, xr, ys, yr, fs, fr) = sems
     nb = nz * ny
     rows, width = h_in.shape
     cols, half = w_in.shape[1:]
@@ -238,20 +238,47 @@
     def grad_share(span):
         return lax.dot_general(h_all[:, span], delta[...], (((0,), (0,)), ((), ())), preferred_element_type=f32)
 
-    order = [lax.rem(z + k, nz) for k in range(1, nz)] + [z]
     slab = ny * cols
+    relay = nz == 4 and slab % 128 == 0
+    turn = jnp.where(z * 2 >= nz, 1, nz - 1)
+    order = [lax.rem(z + turn * k, nz) for k in range(1, nz)] + [z]
+    at_end = (z == 0) | (z == nz - 1)
+    far = jnp.where(z * 2 >= nz, 0, nz - 1)
+    near = jnp.where(z * 2 >= nz, z - 1, z + 1)
+
+    def far_copy(yy):
+        return copy(grad_send.at[wrow(far * ny + yy)], far_in.at[yy], fs.at[yy], fr.at[yy], near * ny + y, v)
+
+    def direct(zz):
+        return jnp.logical_not(at_end & (zz == far))
     if slab % 128 == 0:
         mine = y * cols
         for n in range(nz):
             zz = order[n]
             span = pl.ds(pl.multiple_of(zz * slab, 128), slab)
             share = grad_share(span)
-            grad_send[span, :] = share.astype(bf16)
+            held = relay and n == 1
             if n == nz - 1:
                 grad[...] = share
-            for k in range(ny):
-                if n < nz - 1 or k:
-                    r_copy(zz, turn_y(k)).start()
+            if held:
+                @pl.when(jnp.logical_not(at_end))
+                def _():
+                    far_own[...] = share
+
+                @pl.when(at_end)
+                def _():
+                    grad_send[span, :] = share.astype(bf16)
+                    for k in range(ny):
+                        r_copy(zz, turn_y(k)).start()
+            else:
+                grad_send[span, :] = share.astype(bf16)
+                for k in range(ny):
+                    yy = turn_y(k)
+                    if relay and n == 0:
+                        pl.when(at_end)(lambda: far_copy(yy).start())
+                        pl.when(jnp.logical_not(at_end))(lambda: r_copy(zz, yy).start())
+                    elif n < nz - 1 or k:
+                        r_copy(zz, yy).start()
     else:
         mine = b * cols
         wide = chunk_of(width, 256)
@@ -321,6 +348,30 @@
         over_rows(start_of(kx, ky), core_sum)
         if kx:
             x_copy(kx, ky).start()
+
+    cstep = chunk_of(cols, 64)
+
+    def over_cols(body):
+        def one(r, carry):
+            body(pl.multiple_of(r * cstep, 16))
+            return carry
+
+        lax.fori_loop(0, cols // cstep, one, 0)
+
+    if relay:
+        @pl.when(jnp.logical_not(at_end))
+        def _():
+            for k in range(ny):
+                yy = turn_y(k)
+                far_copy(yy).wait_recv()
+
+                def far_sum(r):
+                    here = pl.ds(pl.multiple_of(yy * cols + r, 16), cstep)
+                    there = pl.ds(pl.multiple_of((far * ny + yy) * cols + r, 16), cstep)
+                    grad_send[there, :] = (far_own[here, :] + far_in[yy, pl.ds(r, cstep), :].astype(f32)).astype(bf16)
+
+                over_cols(far_sum)
+                r_copy(far, yy).start()
 
     for ky in [k % ny for k in range(1, ny + 1)]:
         for kx in range(1, nx):
@@ -339,15 +390,6 @@
         if ky:
             y_copy(ky).start()
 
-    cstep = chunk_of(cols, 64)
-
-    def over_cols(body):
-        def one(r, carry):
-            body(pl.multiple_of(r * cstep, 16))
-            return carry
-
-        lax.fori_loop(0, cols // cstep, one, 0)
-
     def r_got(zz, yy):
         i = zz * ny + yy
         copy(grad_send.at[wrow(i)], r_in.at[zz, yy], rs.at[i], rr.at[i], i, v).wait_recv()
@@ -361,10 +403,9 @@
             head_out[turn_y(k), pl.ds(r, cstep), :] = r_in[z, turn_y(k), pl.ds(r, cstep), :].astype(f32)
 
     over_cols(first_sum)
+    hops = [jnp.where(z * 2 >= nz, lax.rem(z + nz - n, nz), lax.rem(z + n, nz)) for n in range(1, nz)]
     for n in range(1, nz):
-        zz = lax.rem(z + nz - n, nz)
-        for k in range(ny):
-            r_got(zz, turn_y(k))
+        zz = hops[n - 1]
         if n == nz - 1:
             for ky in range(1, ny):
                 y_copy(ky).wait_recv()
@@ -378,7 +419,15 @@
             for k in range(ny):
                 head_out[turn_y(k), pl.ds(r, cstep), :] += r_in[zz, turn_y(k), pl.ds(r, cstep), :].astype(f32)
 
-        over_cols(more_sum)
+        def arrived():
+            for k in range(ny):
+                r_got(zz, turn_y(k))
+            over_cols(more_sum)
+
+        if relay:
+            pl.when(direct(zz))(arrived)
+        else:
+            arrived()
 
     losses = loss_own[...]
     for k in range(1, nb):
@@ -420,8 +469,12 @@
         loss_copy(k).wait_send()
     for n in range(nz):
         for k in range(ny):
-            if n < nz - 1 or k:
-                r_copy(order[n], turn_y(k)).wait_send()
+            yy = turn_y(k)
+            if relay and n == 0:
+                pl.when(at_end)(lambda: far_copy(yy).wait_send())
+                pl.when(jnp.logical_not(at_end))(lambda: r_copy(order[n], yy).wait_send())
+            elif n < nz - 1 or k:
+                r_copy(order[n], yy).wait_send()
 
 
 def local(nb, nv, hidden, head_weight, targets, valid_mask):
@@ -447,11 +500,13 @@
         vm((tokens, width), f32), vm((nx, ny, rows, width), f32),
         vm((lx, ny, rows, width), bf16), vm((lx, ny, rows, width), bf16),
         vm((ly, rows, width), bf16), vm((ly, rows, width), bf16),
+        vm((slab if nz == 4 else 16, half), f32), vm((ny, cols if nz == 4 else 16, half), bf16),
     ]
     sems = [
         dma((2,)), dma((nx + ny,)), dma((nx, ny)), dma((nx, ny)), dma((group,)), dma((nb,)), dma((nb,)),
         dma((ly,)), dma((nb,)), dma((group,)), dma((group,)), dma((group,)), dma((group,)), dma((nb,)), dma((nb,)),
         dma((nb,)), dma((nb,)), dma((nx, ny)), dma((nx, ny)), dma((nx, ny)), dma((nx, ny)), dma((ny,)), dma((ny,)),
+        dma((ny,)), dma((ny,)),
     ]
     whole = pl.BlockSpec(memory_space=vm)
     head_t, hidden_grad, loss = pl.pallas_call(

time: 145 us -> 140 us (0.966)
  the two profiles are of different devices: /device:TPU:24 before, /device:TPU:0 now
where the time goes in v3:
time: 140 us
  Pallas kernels  131 us (94%)
  local copies, waits for them, and re-layouts  7.68 us (5%)
    pallas_call x1, Pallas kernels, local(): pl.pallas_call(functools.partial(kernel, (nz, ny, nx, nv)), out_shape=(ja...  131 us

profile of v3, /device:TPU:0, one launch (start us, length us, event | category | flops | bytes accessed | tf_op | source)
XLA Modules:
  0.0 139.7 jit_solution(9742618913272940516)
XLA Ops:
  0.6 0.7 fusion
  1.3 0.6 broadcast_in_dim.11.code_in
  1.9 2.0 %copy.12 = bf16[56,2,8,384]{3,2,0,1:T(8,128)(2,1)} copy(bf16[56,2,8,384]{3,2,1,0:T(8,128)(2,1)} %bitcast.14) | data formatting | bytes 1376256 | tf_op jit(solution)/shard_map/reshape | solution.py:490
  3.9 130.7 %shard_map.67 = (f32[2,448,384]{2,1,0:T(8,128)}, f32[128,3584]{1,0:T(8,128)}, f32[8,128]{1,0:T(8,128)}) custom-call(bf16[128,3584]{1,0:T(8,128)(2,1)} %h_in.1, bf16[2,448,384]{2,1,0:T(8,128)(2,1)} %bitcast.11, f32[8,128]{1,0:T(8,128)} %broadcast_in_dim.11.code_in), custom_call_target="tpu_custom_call" | custom-call | tf_op jit(solution)/shard_map/pallas_call | solution.py:512
  134.7 0.0 copy-start
  134.7 1.3 slice.3
  136.0 2.5 %copy.10 = f32[2,56,8,384]{3,2,0,1:T(8,128)} copy(f32[2,56,8,384]{3,2,1,0:T(8,128)} %bitcast.13) | data formatting | bytes 2752512 | tf_op jit(solution)/shard_map/reshape | solution.py:525
  138.5 0.0 copy-done
  138.5 1.2 copy.14
Async XLA Ops:
  134.7 3.9 %copy-start = (f32[128,3584]{1,0:T(8,128)S(1)}, f32[128,3584]{1,0:T(8,128)}, u32[]{:S(2)}) copy-start(f32[128,3584]{1,0:T(8,128)} %get-tuple-element.13) | copy-start | bytes 5505028
